TPU v7x, 32 devices: a whole 2x2x4 slice. The times are simulated.
32 devices in a mesh: seq: 8 (over y, x, core), head: 4 (over z).
Axes of the slice: x: 2, y: 2, z: 4, core: 2. Of those that a mesh axis runs over, the one named last changes fastest.
Arguments:
- queries: bfloat16 [1536, 2048], P('seq', 'head'), may hold values from -6 to 6, as said below
- keys: bfloat16 [1536, 256], P('seq'), may hold values from -6 to 6, as said below
- values: bfloat16 [1536, 256], P('seq'), may hold values from -6 to 6
- out_weight: bfloat16 [2048, 8192], P('head'), may hold values from -0.25 to 0.25
- doc_lengths: int32 [48], replicated, may hold values from 1 to 384, 1536 in all
- pair_ids: int32 [48], replicated, may hold values from 0 to 23, never falling along the last dimension, each value on 1 to 3 neighbouring positions
- block_plan: int32 [32], replicated, may hold values from 0 to 31, as said below
Outputs:
- projected: bfloat16 [1536, 8192], P(('seq', 'head'))
Inputs may be any that keep to these rules, and one draw needn't show every extreme that they name: Entries of queries lie in the range given. Entries of keys lie in the range given. `doc_lengths`: the lengths sum to 1536. `pair_ids`: never falling; every pair 0 to 23 holds one to three consecutive documents. `block_plan`: A permutation of the 32 blocks of 48 tokens, numbered along the row. The 4 consecutive slots of one seq index hold blocks from 4 different seq indices, and the 4 blocks of one seq index go to 4 different seq indices.
All inputs are finite; a program needn't handle non-finite values.
Results may differ from a plain program's by a relative error of at most 0.015.
Values may be sent and summed in bfloat16 or wider, within the bound.
A program may use at most 64 MiB of HBM per device.

v0:
```python
import math
import jax
import jax.numpy as jnp
from jax import lax
from jax.sharding import PartitionSpec as P

D_HEAD = 128
NEGATIVE = -1e30


def token_docs(positions, doc_lengths):
    doc_ends = jnp.cumsum(doc_lengths)
    return jnp.sum((doc_ends[None, :] <= positions[:, None]).astype(jnp.int32), axis=1)


def pair_firsts(docs, pair_ids):
    doc_range = jnp.arange(pair_ids.shape[0], dtype=jnp.int32)
    own_pair = jnp.sum(jnp.where(docs[:, None] == doc_range[None, :], pair_ids[None, :], 0), axis=1)
    return jnp.sum((pair_ids[None, :] < own_pair[:, None]).astype(jnp.int32), axis=1)


def largest_divisor(total_rows, ceiling):
    return max(
        (
            candidate
            for candidate in range(1, min(total_rows, ceiling) + 1)
            if total_rows % candidate == 0
        )
    )


def attend(query_rows, positions, keys, values, doc_lengths, pair_ids):
    head_size = keys.shape[1]
    token_count = query_rows.shape[0]
    query_heads = query_rows.shape[1] // head_size
    shaped_queries = query_rows.reshape(token_count, query_heads, head_size)
    query_docs = token_docs(positions, doc_lengths)
    query_firsts = pair_firsts(query_docs, pair_ids)
    doc_range = jnp.arange(doc_lengths.shape[0], dtype=jnp.int32)
    pair_begin = jnp.sum(
        jnp.where(doc_range[None, :] < query_firsts[:, None], doc_lengths[None, :], 0), axis=1
    )
    lowest = jnp.min(pair_begin)
    highest = jnp.max(positions)
    scale = 1.0 / math.sqrt(head_size)

    def update(softmax_state, key_block, value_block, block_start):
        key_pos = block_start + jnp.arange(key_block.shape[0], dtype=jnp.int32)
        needed = (block_start <= highest) & (block_start + key_block.shape[0] > lowest)

        def compute(current):
            running_max, denominator, weighted = current
            key_docs = token_docs(key_pos, doc_lengths)
            allowed = (key_pos[None, :] <= positions[:, None]) & (
                (key_docs[None, :] == query_docs[:, None])
                | (key_docs[None, :] == query_firsts[:, None])
            )
            scores = (
                jnp.einsum(
                    "qhd,kd->hqk", shaped_queries, key_block, preferred_element_type=jnp.float32
                )
                * scale
            )
            newest = jnp.maximum(
                running_max, jnp.max(jnp.where(allowed[None], scores, NEGATIVE), axis=2)
            )
            weights = jnp.where(allowed[None], jnp.exp(scores - newest[:, :, None]), 0.0)
            factor = jnp.exp(running_max - newest)
            denominator = denominator * factor + jnp.sum(weights, axis=2)
            weighted = weighted * factor[:, :, None] + jnp.einsum(
                "hqk,kd->hqd",
                weights.astype(jnp.bfloat16),
                value_block,
                preferred_element_type=jnp.float32,
            )
            return (newest, denominator, weighted)

        def unchanged(current):
            return current

        return lax.cond(needed, compute, unchanged, softmax_state)

    initial = (
        jnp.full((query_heads, token_count), NEGATIVE, jnp.float32),
        jnp.zeros((query_heads, token_count), jnp.float32),
        jnp.zeros((query_heads, token_count, head_size), jnp.float32),
    )
    key_rows = lax.all_gather(keys, "seq", axis=0, tiled=True)
    value_rows = lax.all_gather(values, "seq", axis=0, tiled=True)
    row_total = key_rows.shape[0]
    block_rows = largest_divisor(row_total, 1024)
    block_count = row_total // block_rows
    stacked = (
        key_rows.reshape(block_count, block_rows, head_size),
        value_rows.reshape(block_count, block_rows, head_size),
        jnp.int32(0) + block_rows * jnp.arange(block_count, dtype=jnp.int32),
    )

    def advance(carried, block_item):
        return (update(carried, block_item[0], block_item[1], block_item[2]), None)

    result_state, unused_out = lax.scan(advance, initial, stacked)
    running_max, denominator, weighted = result_state
    attended = weighted / denominator[:, :, None]
    return (
        attended.transpose(1, 0, 2)
        .reshape(token_count, query_heads * head_size)
        .astype(jnp.bfloat16)
    )


def on_device(queries, keys, values, out_weight, doc_lengths, pair_ids, block_plan):
    seq_count = lax.axis_size("seq")
    my_seq = lax.axis_index("seq")
    shared_head = lax.axis_index("head") // 2
    key_rows = lax.dynamic_slice_in_dim(keys, shared_head * D_HEAD, D_HEAD, 1)
    value_rows = lax.dynamic_slice_in_dim(values, shared_head * D_HEAD, D_HEAD, 1)
    slots_here = seq_count // 2
    tok_rows = queries.shape[0]
    row_width = queries.shape[1]
    block_rows = tok_rows // slots_here
    slot_total = block_plan.shape[0]
    local_ids = my_seq * slots_here + jnp.arange(slots_here, dtype=jnp.int32)
    plan_rows = lax.dynamic_slice_in_dim(block_plan, my_seq * slots_here, slots_here, 0)
    planned_pos = (
        plan_rows[:, None] * block_rows + jnp.arange(block_rows, dtype=jnp.int32)[None, :]
    ).reshape(-1)
    slot_range = jnp.arange(slot_total, dtype=jnp.int32)
    target_slot = jnp.sum(
        jnp.where(block_plan[None, :] == local_ids[:, None], slot_range[None, :], 0), axis=1
    )
    device_range = jnp.arange(seq_count, dtype=jnp.int32)
    send_table = ((target_slot // slots_here)[:, None] == device_range[None, :]).astype(
        jnp.bfloat16
    )
    take_table = ((plan_rows // slots_here)[:, None] == device_range[None, :]).astype(jnp.bfloat16)
    blocked = queries.reshape(slots_here, block_rows, row_width)
    arrived = lax.all_to_all(
        jnp.einsum("bn,bkw->nkw", send_table, blocked, preferred_element_type=jnp.float32).astype(
            jnp.bfloat16
        ),
        "seq",
        split_axis=0,
        concat_axis=0,
        tiled=True,
    )
    chosen = jnp.einsum("bn,nkw->bkw", take_table, arrived, preferred_element_type=jnp.float32)
    attended = attend(
        chosen.astype(jnp.bfloat16).reshape(tok_rows, row_width),
        planned_pos,
        key_rows,
        value_rows,
        doc_lengths,
        pair_ids,
    )
    return lax.psum_scatter(
        jnp.dot(attended, out_weight, preferred_element_type=jnp.float32).astype(jnp.bfloat16),
        "head",
        scatter_dimension=0,
        tiled=True,
    )


def solution(mesh):
    return jax.shard_map(
        on_device,
        mesh=mesh,
        in_specs=(P("seq", "head"), P("seq", None), P("seq", None), P("head", None), P(), P(), P()),
        out_specs=P(("seq", "head"), None),
        check_vma=False,
    )
```

profile of v0, /device:TPU:0, one launch (start us, length us, event | category | flops | bytes accessed | tf_op | source)
XLA Modules:
  0.0 128.1 jit_solution(16628329436122712984)
XLA Ops:
  6.5 0.9 select_reduce_fusion.2
  7.9 0.9 copy.26
  8.7 5.2 %all-to-all-start = ((bf16[8,48,512]{2,1,0:T(8,128)(2,1)}), bf16[8,48,512]{2,1,0:T(8,128)(2,1)S(1)}, u32[]{:S(2)}, u32[]{:S(2)}) async-start(bf16[8,48,512]{2,1,0:T(8,128)(2,1)} %copy.26), calls=%async_computation | async-start | bytes 786432 | tf_op jit(solution)/shard_map/all_to_all | solution.py:138
  14.0 0.7 and_select_fusion.1
  14.7 0.8 iota_add_fusion
  15.6 0.7 copy.24
  16.6 0.7 select_reduce_fusion.1
  17.4 0.7 convert_reduce_fusion.1
  18.1 0.7 select_reduce_fusion
  18.9 10.0 %all_gather.7 = bf16[1536,128]{1,0:T(8,128)(2,1)S(1)} all-gather(bf16[192,128]{1,0:T(8,128)(2,1)S(1)} %constant_dynamic-slice_fusion), channel_id=1, replica_groups=mesh['seq'=8,'head'=4] {'seq'}, dimensions={0}, use_global_device_ids=true | all-gather | bytes 442368 | tf_op jit(solution)/shard_map/all_gather | solution.py:89
  29.6 9.5 %all_gather.6 = bf16[1536,128]{1,0:T(8,128)(2,1)S(1)} all-gather(bf16[192,128]{1,0:T(8,128)(2,1)S(1)} %constant_dynamic-slice_fusion.1), channel_id=1, replica_groups=mesh['seq'=8,'head'=4] {'seq'}, dimensions={0}, use_global_device_ids=true | all-gather | bytes 442368 | tf_op jit(solution)/shard_map/all_gather | solution.py:88
  39.6 13.9 %while.15 = (s32[]{:T(128)}, f32[4,192]{1,0:T(4,128)S(1)}, f32[4,192]{1,0:T(4,128)S(1)}, f32[4,192,128]{2,1,0:T(8,128)S(1)}, s32[2]{0:T(128)S(1)}, /*index=5*/s3...) while((s32[]{:T(128)}, f32[4,192]{1,0:T(4,128)S(1)}, ...), condition=%wide.region_15.16_spmd.clone, body=%wide.region_8.15_spmd.clone.sunk | while | flops 309526400 | bytes 9124563 | solution.py:102
  42.8 3.8 %conditional.3 = ((f32[4,192]{1,0:T(4,128)S(1)}, f32[4,192]{1,0:T(4,128)S(1)}, f32[4,192,128]{2,1,0:T(8,128)S(1)})) conditional(s32[]{:T(128)} %convert_element_type.62, (f32[4,192]{1,0:T(4,128)S(1)}, f32[4,192]{1,0:T(4,128)S(1)}, f32[4,192,128]{2,1,0:T(8,128)S(1)}) %tuple.43, (s32[]{:T(128)}, s32[768]{0:T(1024)S(1)}, s32[4]{0:T(128)S(1)}, ...), branch_computations={%region_9.9_spmd, %region_10.14_spmd} | conditional | flops 309526400 | bytes 9120388 | solution.py:81
  42.8 0.7 broadcast_add_fusion
  44.2 0.7 fusion.2
  44.9 0.8 fusion.6
  45.7 0.8 convolution_add_fusion
  49.7 3.8 %conditional.3 = ((f32[4,192]{1,0:T(4,128)S(1)}, f32[4,192]{1,0:T(4,128)S(1)}, f32[4,192,128]{2,1,0:T(8,128)S(1)})) conditional(s32[]{:T(128)} %convert_element_type.62, (f32[4,192]{1,0:T(4,128)S(1)}, f32[4,192]{1,0:T(4,128)S(1)}, f32[4,192,128]{2,1,0:T(8,128)S(1)}) %tuple.43, (s32[]{:T(128)}, s32[768]{0:T(1024)S(1)}, s32[4]{0:T(128)S(1)}, ...), branch_computations={%region_9.9_spmd, %region_10.14_spmd} | conditional | flops 309526400 | bytes 9120388 | solution.py:81
  49.8 0.7 broadcast_add_fusion
  51.2 0.7 fusion.2
  51.9 0.8 fusion.6
  52.6 0.8 convolution_add_fusion
  53.5 6.9 %convolution_convert_fusion = bf16[192,8192]{1,0:T(8,128)(2,1)} fusion(bf16[512,8192]{1,0:T(8,128)(2,1)} %param.14, f32[4,192,128]{2,1,0:T(8,128)S(1)} %get-tuple-element.191, f32[4,192]{1,0:T(4,128)S(1)} %get-tuple-element.192), kind=kOutput, calls=%fused_computation.27 | convolution fusion | flops 1612382208 | bytes 11930624 | tf_op jit(solution)/shard_map/dot_general | solution.py:157
  60.4 60.8 %reduce-scatter.2.cloned.1.call-done = bf16[48,8192]{1,0:T(8,128)(2,1)} async-done(((bf16[192,8192]{1,0:T(8,128)(2,1)}), bf16[48,8192]{1,0:T(8,128)(2,1)}) %reduce-scatter.2.cloned.1.call-update) | async-done | bytes 786448 | tf_op jit(solution)/shard_map/reduce_scatter | solution.py:156
  (55 shorter events, 4.7 us)
Async XLA Ops:
  6.5 0.9 copy-start
  6.5 12.3 %copy-start.2 = (bf16[192,256]{1,0:T(8,128)(2,1)S(1)}, bf16[192,256]{1,0:T(8,128)(2,1)}, u32[]{:S(2)}) copy-start(bf16[192,256]{1,0:T(8,128)(2,1)} %param.13) | copy-start | bytes 294916
  6.5 23.0 %copy-start.3 = (bf16[192,256]{1,0:T(8,128)(2,1)S(1)}, bf16[192,256]{1,0:T(8,128)(2,1)}, u32[]{:S(2)}) copy-start(bf16[192,256]{1,0:T(8,128)(2,1)} %param.12) | copy-start | bytes 294916
  7.9 31.8 %copy-start.1 = (s32[48]{0:T(128)S(1)}, s32[48]{0:T(128)}, u32[]{:S(2)}) copy-start(s32[48]{0:T(128)} %param.15) | copy-start | bytes 580
  8.7 30.3 %all-to-all-start = ((bf16[8,48,512]{2,1,0:T(8,128)(2,1)}), bf16[8,48,512]{2,1,0:T(8,128)(2,1)S(1)}, u32[]{:S(2)}, u32[]{:S(2)}) async-start(bf16[8,48,512]{2,1,0:T(8,128)(2,1)} %copy.26), calls=%async_computation | async-start | bytes 786432 | tf_op jit(solution)/shard_map/all_to_all | solution.py:138
  13.9 107.4 %reduce-scatter.2.cloned.1.call-start = ((), (), s32[]{:S(2)}) async-start(), calls=%async_computation.2 | async-start | bytes 3932160 | tf_op jit(solution)/shard_map/reduce_scatter | solution.py:156
Sparse Core Ops, SparseCore 0:
  60.6 60.6 reduce-scatter.1
where the time goes:
time: 129 us; the launch traced here: 128 us
  waiting for transfers between devices  60.9 us (47%)
  blocking collectives  19.5 us (15%)
  between operations  13.5 us (10%)
  matrix products  10.7 us (8%)
  other arithmetic  9.6 us (7%)
  loops' own time  5.26 us (4%)
  starting transfers between devices  5.23 us (4%)
  local copies, waits for them, and re-layouts  3.44 us (3%)
    reduce_scatter x1, waiting for transfers between devices, on_device(): lax.psum_scatter(jnp.dot(attended, out_weight, preferred_element_type=jnp...  60.8 us
    all_gather x1, blocking collectives, attend(): value_rows = lax.all_gather(values, 'seq', axis=0, tiled=True)  10 us
    all_gather x1, blocking collectives, attend(): key_rows = lax.all_gather(keys, 'seq', axis=0, tiled=True)  9.51 us
    dot_general x1, matrix products, on_device(): jnp.dot(attended, out_weight, preferred_element_type=jnp.float32)  6.91 us
    all_to_all x1, starting transfers between devices, on_device(): lax.all_to_all(jnp.einsum('bn,bkw->nkw', send_table, blocked, preferred_e...  5.2 us
    another operation x1, loops' own time, attend(): result_state, unused_out = lax.scan(advance, initial, stacked)  5.15 us
  transfers between devices with their start and end apart: 2, of which 1 were waited for; matrix products, arithmetic and copies ran while one was open for 4% of the time, Pallas kernels for 0%

commit v1 on v0

--- a/solution.py
+++ b/solution.py
@@ -85,8 +85,17 @@
         jnp.zeros((query_heads, token_count), jnp.float32),
         jnp.zeros((query_heads, token_count, head_size), jnp.float32),
     )
-    key_rows = lax.all_gather(keys, "seq", axis=0, tiled=True)
-    value_rows = lax.all_gather(values, "seq", axis=0, tiled=True)
+
+    def turn_lanes(state, chunk, bus_axis):
+        return jnp.split(
+            lax.all_gather(
+                jnp.concatenate([state, chunk], axis=1), axis=0, tiled=True, axis_name=bus_axis
+            ),
+            [state.shape[1]],
+            axis=1,
+        )
+
+    key_rows, value_rows = turn_lanes(keys, values, "seq")
     row_total = key_rows.shape[0]
     block_rows = largest_divisor(row_total, 1024)
     block_count = row_total // block_rows

time: 129 us -> 120 us (0.930)
  blocking collectives: 19.5 us -> 12.9 us
  other arithmetic: 9.6 us -> 7.02 us
    all_gather x2 -> x1, blocking collectives: 19.5 us -> 12.9 us  [turn_lanes(): lax.all_gather(jnp.concatenate([state, chunk], axis=1), axis=0, tiled=Tru...]
  transfers between devices with their start and end apart: 2 -> 2, of which waited for: 1 -> 1; matrix products, arithmetic and copies ran while one was open for 4% -> 3% of each run, Pallas kernels for 0% -> 0%
where the time goes in v1:
time: 120 us; the launch traced here: 119 us
  waiting for transfers between devices  60.9 us (51%)
  between operations  13.5 us (11%)
  blocking collectives  12.9 us (11%)
  matrix products  10.7 us (9%)
  other arithmetic  7.02 us (6%)
  loops' own time  5.26 us (4%)
  starting transfers between devices  5.23 us (4%)
  local copies, waits for them, and re-layouts  3.65 us (3%)
    reduce_scatter x1, waiting for transfers between devices, on_device(): lax.psum_scatter(jnp.dot(attended, out_weight, preferred_element_type=jnp...  60.8 us
    all_gather x1, blocking collectives, turn_lanes(): lax.all_gather(jnp.concatenate([state, chunk], axis=1), axis=0, tiled=Tru...  12.9 us
    dot_general x1, matrix products, on_device(): jnp.dot(attended, out_weight, preferred_element_type=jnp.float32)  6.91 us
    all_to_all x1, starting transfers between devices, on_device(): lax.all_to_all(jnp.einsum('bn,bkw->nkw', send_table, blocked, preferred_e...  5.2 us
    another operation x1, loops' own time, attend(): result_state, unused_out = lax.scan(advance, initial, stacked)  5.15 us
  transfers between devices with their start and end apart: 2, of which 1 were waited for; matrix products, arithmetic and copies ran while one was open for 3% of the time, Pallas kernels for 0%

profile of v1, /device:TPU:0, one launch (start us, length us, event | category | flops | bytes accessed | tf_op | source)
XLA Modules:
  0.0 119.2 jit_solution(6583112105385251287)
XLA Ops:
  6.5 0.9 select_reduce_fusion.2
  7.5 0.4 convolution_convert_fusion.1
  7.9 0.9 copy.26
  8.7 5.2 %all-to-all-start = ((bf16[8,48,512]{2,1,0:T(8,128)(2,1)}), bf16[8,48,512]{2,1,0:T(8,128)(2,1)S(1)}, u32[]{:S(2)}, u32[]{:S(2)}) async-start(bf16[8,48,512]{2,1,0:T(8,128)(2,1)} %copy.26), calls=%async_computation | async-start | bytes 786432 | tf_op jit(solution)/shard_map/all_to_all | solution.py:147
  14.0 0.8 constant_dynamic-slice_fusion
  14.8 12.9 %all_gather.3 = bf16[1536,256]{1,0:T(8,128)(2,1)S(1)} all-gather(bf16[192,256]{1,0:T(8,128)(2,1)S(1)} %pad_maximum_fusion), channel_id=1, replica_groups=mesh['seq'=8,'head'=4] {'seq'}, dimensions={0}, use_global_device_ids=true | all-gather | bytes 884736 | tf_op jit(solution)/shard_map/all_gather | solution.py:91
  27.8 0.8 iota_add_fusion
  29.4 0.6 reduce_min.9
  30.1 0.4 convolution_convert_fusion.2
  30.6 13.9 %while.15 = (s32[]{:T(128)}, f32[4,192]{1,0:T(4,128)S(1)}, f32[4,192]{1,0:T(4,128)S(1)}, f32[4,192,128]{2,1,0:T(8,128)S(1)}, s32[2]{0:T(128)S(1)}, /*index=5*/s3...) while((s32[]{:T(128)}, f32[4,192]{1,0:T(4,128)S(1)}, ...), condition=%wide.region_15.16_spmd.clone, body=%wide.region_8.15_spmd.clone.sunk | while | flops 309526400 | bytes 9124563 | solution.py:111
  30.6 0.6 dynamic_slice.49
  33.8 3.8 %conditional.3 = ((f32[4,192]{1,0:T(4,128)S(1)}, f32[4,192]{1,0:T(4,128)S(1)}, f32[4,192,128]{2,1,0:T(8,128)S(1)})) conditional(s32[]{:T(128)} %convert_element_type.62, (f32[4,192]{1,0:T(4,128)S(1)}, f32[4,192]{1,0:T(4,128)S(1)}, f32[4,192,128]{2,1,0:T(8,128)S(1)}) %tuple.45, (s32[]{:T(128)}, s32[768]{0:T(1024)S(1)}, s32[4]{0:T(128)S(1)}, ...), branch_computations={%region_9.9_spmd, %region_10.14_spmd} | conditional | flops 309526400 | bytes 9120388 | solution.py:81
  33.8 0.7 broadcast_add_fusion
  35.2 0.7 fusion.2
  35.9 0.8 fusion.6
  36.7 0.9 convolution_add_fusion
  37.6 0.6 dynamic_slice.49
  40.7 3.8 %conditional.3 = ((f32[4,192]{1,0:T(4,128)S(1)}, f32[4,192]{1,0:T(4,128)S(1)}, f32[4,192,128]{2,1,0:T(8,128)S(1)})) conditional(s32[]{:T(128)} %convert_element_type.62, (f32[4,192]{1,0:T(4,128)S(1)}, f32[4,192]{1,0:T(4,128)S(1)}, f32[4,192,128]{2,1,0:T(8,128)S(1)}) %tuple.45, (s32[]{:T(128)}, s32[768]{0:T(1024)S(1)}, s32[4]{0:T(128)S(1)}, ...), branch_computations={%region_9.9_spmd, %region_10.14_spmd} | conditional | flops 309526400 | bytes 9120388 | solution.py:81
  40.8 0.7 broadcast_add_fusion
  42.2 0.7 fusion.2
  42.9 0.8 fusion.6
  43.7 0.9 convolution_add_fusion
  44.6 6.9 %convolution_convert_fusion = bf16[192,8192]{1,0:T(8,128)(2,1)} fusion(bf16[512,8192]{1,0:T(8,128)(2,1)} %param.14, f32[4,192,128]{2,1,0:T(8,128)S(1)} %get-tuple-element.191, f32[4,192]{1,0:T(4,128)S(1)} %get-tuple-element.192), kind=kOutput, calls=%fused_computation.27 | convolution fusion | flops 1612382208 | bytes 11930624 | tf_op jit(solution)/shard_map/dot_general | solution.py:166
  51.5 60.8 %reduce-scatter.2.cloned.1.call-done = bf16[48,8192]{1,0:T(8,128)(2,1)} async-done(((bf16[192,8192]{1,0:T(8,128)(2,1)}), bf16[48,8192]{1,0:T(8,128)(2,1)}) %reduce-scatter.2.cloned.1.call-update) | async-done | bytes 786448 | tf_op jit(solution)/shard_map/reduce_scatter | solution.py:165
  (55 shorter events, 2.7 us)
Async XLA Ops:
  6.5 0.9 copy-start
  6.5 21.2 %copy-start.3 = (s32[32]{0:T(128)S(1)}, s32[32]{0:T(128)}, u32[]{:S(2)}) copy-start(s32[32]{0:T(128)} %param.17) | copy-start | bytes 388
  6.5 22.2 %copy-start.1 = (s32[48]{0:T(128)S(1)}, s32[48]{0:T(128)}, u32[]{:S(2)}) copy-start(s32[48]{0:T(128)} %param.15) | copy-start | bytes 580
  6.5 22.5 %copy-start.2 = (s32[48]{0:T(128)S(1)}, s32[48]{0:T(128)}, u32[]{:S(2)}) copy-start(s32[48]{0:T(128)} %param.16) | copy-start | bytes 580
  8.7 21.3 %all-to-all-start = ((bf16[8,48,512]{2,1,0:T(8,128)(2,1)}), bf16[8,48,512]{2,1,0:T(8,128)(2,1)S(1)}, u32[]{:S(2)}, u32[]{:S(2)}) async-start(bf16[8,48,512]{2,1,0:T(8,128)(2,1)} %copy.26), calls=%async_computation | async-start | bytes 786432 | tf_op jit(solution)/shard_map/all_to_all | solution.py:147
  13.9 98.4 %reduce-scatter.2.cloned.1.call-start = ((), (), s32[]{:S(2)}) async-start(), calls=%async_computation.2 | async-start | bytes 3932160 | tf_op jit(solution)/shard_map/reduce_scatter | solution.py:165
Sparse Core Ops, SparseCore 0:
  51.6 60.6 reduce-scatter.1
